TPU v7x, 32 devices: a whole 2x2x4 slice. The times are simulated.
32 devices in a mesh: row: 4 (over z), col: 8 (over y, x, core).
Axes of the slice: x: 2, y: 2, z: 4, core: 2. Of those that a mesh axis runs over, the one named last changes fastest.
Arguments:
- tokens: bfloat16 [2048, 2048], P(('row', 'col')), may hold values from -6 to 6
- timestep: int32 [1], replicated, may hold values from 0 to 999
- mod_weight: float32 [256, 2048], replicated, may hold values from -0.375 to 0.375
- qkv_weight: bfloat16 [3, 2048, 2048], P(None, None, 'col'), may hold values from -0.125 to 0.125
- attn_scale: float32 [16], P('col'), may hold values from 4 to 40
- out_weight: bfloat16 [2048, 2048], P('col'), may hold values from -0.5 to 0.5
- grad_update: bfloat16 [2048, 2048], P(('row', 'col')), may hold values from -6 to 6
Outputs:
- update: bfloat16 [2048, 2048], P(('row', 'col'))
- grad_tokens: bfloat16 [2048, 2048], P(('row', 'col'))
- grad_qkv: float32 [3, 2048, 2048], P(None, 'row', 'col')
- grad_out: float32 [2048, 2048], P('col', 'row')
All inputs are finite; a program needn't handle non-finite values.
Results may differ from a plain program's by a relative error of at most 0.018.
Values may be sent and summed in bfloat16 or wider, within the bound.
A program may use at most 128 MiB of HBM per device.

v0:
```python
import math
import jax
import jax.numpy as jnp
from jax import lax
from jax.sharding import PartitionSpec as P

epsilon = 1e-06


def embed(timestep, count):
    index = jnp.arange(count, dtype=jnp.float32)
    freqs = jnp.exp(-math.log(10000.0) * index / count)
    angles = timestep.astype(jnp.float32)[0] * freqs
    return jnp.concatenate([jnp.cos(angles), jnp.sin(angles)])


def unit_rows(values):
    factor = lax.rsqrt(jnp.mean(values * values, -1, keepdims=True) + epsilon)
    return (values * factor, factor)


def unit_grad(grad_unit, unit, factor):
    return factor * (grad_unit - unit * jnp.mean(grad_unit * unit, -1, keepdims=True))


def split_blocks(array, size):
    return array.reshape((array.shape[0] // size, size) + array.shape[1:])


def per_device(tokens, timestep, mod_weight, qkv_weight, attn_scale, out_weight, grad_update):
    tok_dev, width = tokens.shape
    heads_here = attn_scale.shape[0]
    inner = qkv_weight.shape[2]
    head_dim = inner // heads_here
    span = tok_dev * lax.axis_size("col")
    coeff = attn_scale / head_dim
    embedded = embed(timestep, mod_weight.shape[0] // 2)
    gain = 1.0 + jnp.sum(embedded[:, None] * mod_weight, 0)
    tok_float = tokens.astype(jnp.float32)
    rstd = lax.rsqrt(jnp.mean(tok_float * tok_float, -1, keepdims=True) + epsilon)
    normed = tok_float * rstd
    hidden = (normed * gain).astype(jnp.bfloat16)
    group = lax.all_gather(hidden, "col", axis=0, tiled=True)
    raw = jnp.einsum("sd,kdh->ksh", group, qkv_weight, preferred_element_type=jnp.float32)
    query_unit, query_factor = unit_rows(raw[0].reshape(span, heads_here, head_dim))
    key_unit, key_factor = unit_rows(raw[1].reshape(span, heads_here, head_dim))
    queries = query_unit.astype(jnp.bfloat16)
    key_heads = key_unit.astype(jnp.bfloat16)
    value_heads = raw[2].astype(jnp.bfloat16).reshape(span, heads_here, head_dim)
    start_state = (
        jnp.zeros((heads_here, span), jnp.float32),
        jnp.zeros((span, heads_here, head_dim), jnp.float32),
    )
    carry = start_state
    key_piece = lax.all_gather(key_heads, "row", axis=0, tiled=True)
    value_piece = lax.all_gather(value_heads, "row", axis=0, tiled=True)
    size = math.gcd(key_piece.shape[0], 512)

    def attend_step(state, block):
        key_block, value_block = block
        scores = (
            jnp.einsum("qhd,khd->hqk", queries, key_block, preferred_element_type=jnp.float32)
            * coeff[:, None, None]
        )
        weights = jnp.exp(scores - attn_scale[:, None, None])
        totals = state[0] + jnp.sum(weights, -1)
        mixed = state[1] + jnp.einsum(
            "hqk,khd->qhd",
            weights.astype(jnp.bfloat16),
            value_block,
            preferred_element_type=jnp.float32,
        )
        return ((totals, mixed), None)

    carry, unused = lax.scan(
        attend_step, carry, (split_blocks(key_piece, size), split_blocks(value_piece, size))
    )
    totals, mixed = carry
    attended_heads = (mixed / totals.T[:, :, None]).astype(jnp.bfloat16)
    attended = attended_heads.reshape(span, inner)
    rows = attended
    update = lax.psum_scatter(
        jnp.dot(rows, out_weight, preferred_element_type=jnp.float32).astype(jnp.bfloat16),
        "col",
        scatter_dimension=0,
        tiled=True,
    )
    grad_group = lax.all_gather(grad_update, "col", axis=0, tiled=True)
    out_part = lax.dot_general(
        attended, grad_group, (((0,), (0,)), ((), ())), preferred_element_type=jnp.float32
    )
    grad_out = lax.psum_scatter(
        out_part.astype(jnp.bfloat16), "row", scatter_dimension=1, tiled=True
    ).astype(jnp.float32)
    grad_attended = lax.dot_general(
        grad_group, out_weight, (((1,), (1,)), ((), ())), preferred_element_type=jnp.float32
    ).astype(jnp.bfloat16)
    grad_heads = grad_attended.reshape(span, heads_here, head_dim)
    delta = jnp.sum(grad_heads.astype(jnp.float32) * attended_heads.astype(jnp.float32), -1)
    inverse = 1.0 / totals

    def pair_terms(query_rows, grad_rows, inverse_rows, delta_rows, key_block, value_block):
        scores = (
            jnp.einsum("qhd,khd->hqk", query_rows, key_block, preferred_element_type=jnp.float32)
            * coeff[:, None, None]
        )
        probs = jnp.exp(scores - attn_scale[:, None, None]) * inverse_rows[:, :, None]
        dprobs = jnp.einsum(
            "qhd,khd->hqk", grad_rows, value_block, preferred_element_type=jnp.float32
        )
        dscores = (probs * (dprobs - delta_rows[:, :, None]) * coeff[:, None, None]).astype(
            jnp.bfloat16
        )
        return (probs, dscores)

    empty_own = jnp.zeros((span, heads_here, head_dim), jnp.float32)
    carry = empty_own
    key_piece = lax.all_gather(key_heads, "row", axis=0, tiled=True)
    value_piece = lax.all_gather(value_heads, "row", axis=0, tiled=True)
    size = math.gcd(key_piece.shape[0], 512)

    def query_step(state, block):
        key_block, value_block = block
        probs, dscores = pair_terms(queries, grad_heads, inverse, delta.T, key_block, value_block)
        return (
            state
            + jnp.einsum("hqk,khd->qhd", dscores, key_block, preferred_element_type=jnp.float32),
            None,
        )

    carry, unused = lax.scan(
        query_step, carry, (split_blocks(key_piece, size), split_blocks(value_piece, size))
    )
    grad_query = carry
    all_inverse, all_delta = (
        lax.all_gather(inverse.T, "row", axis=0, tiled=True),
        lax.all_gather(delta, "row", axis=0, tiled=True),
    )
    carry = (empty_own, empty_own)
    query_piece = lax.all_gather(queries, "row", axis=0, tiled=True)
    grad_piece = lax.all_gather(grad_heads, "row", axis=0, tiled=True)
    count = query_piece.shape[0]
    size = math.gcd(count, 512)

    def key_step(state, block):
        query_block, grad_block, inverse_block, delta_block = block
        probs, dscores = pair_terms(
            query_block, grad_block, inverse_block.T, delta_block.T, key_heads, value_heads
        )
        grad_key = state[0] + jnp.einsum(
            "hqk,qhd->khd", dscores, query_block, preferred_element_type=jnp.float32
        )
        grad_value = state[1] + jnp.einsum(
            "hqk,qhd->khd",
            probs.astype(jnp.bfloat16),
            grad_block,
            preferred_element_type=jnp.float32,
        )
        return ((grad_key, grad_value), None)

    carry, unused = lax.scan(
        key_step,
        carry,
        (
            split_blocks(query_piece, size),
            split_blocks(grad_piece, size),
            split_blocks(all_inverse, size),
            split_blocks(all_delta, size),
        ),
    )
    grad_key, grad_value = carry
    grad_q = (
        unit_grad(grad_query, query_unit, query_factor).astype(jnp.bfloat16).reshape(span, inner)
    )
    grad_k = unit_grad(grad_key, key_unit, key_factor).astype(jnp.bfloat16).reshape(span, inner)
    grad_v = grad_value.astype(jnp.bfloat16).reshape(span, inner)
    grad_raw = jnp.stack([grad_q, grad_k, grad_v])
    qkv_part = jnp.einsum("sd,ksh->kdh", group, grad_raw, preferred_element_type=jnp.float32)
    grad_qkv = lax.psum_scatter(
        qkv_part.astype(jnp.bfloat16), "row", scatter_dimension=1, tiled=True
    ).astype(jnp.float32)
    rows = grad_raw
    grad_hidden = lax.psum_scatter(
        jnp.einsum("ksh,kdh->sd", rows, qkv_weight, preferred_element_type=jnp.float32).astype(
            jnp.bfloat16
        ),
        "col",
        scatter_dimension=0,
        tiled=True,
    ).astype(jnp.float32)
    grad_normed = grad_hidden * gain
    grad_tokens = (
        rstd * (grad_normed - normed * jnp.mean(grad_normed * normed, -1, keepdims=True))
    ).astype(jnp.bfloat16)
    return (update, grad_tokens, grad_qkv, grad_out)


def solution(mesh):
    placed = (
        P(("row", "col"), None),
        P(),
        P(),
        P(None, None, "col"),
        P("col"),
        P("col", None),
        P(("row", "col"), None),
    )
    return jax.shard_map(
        per_device,
        mesh=mesh,
        in_specs=placed,
        out_specs=(
            P(("row", "col"), None),
            P(("row", "col"), None),
            P(None, "row", "col"),
            P("col", "row"),
        ),
        check_vma=False,
    )
```

profile of v0, /device:TPU:0, one launch (start us, length us, event | category | flops | bytes accessed | tf_op | source)
XLA Modules:
  0.0 422.1 jit_solution(2159010349905390229)
XLA Ops:
  11.1 30.6 %all-gather.7.cloned.1.call-done = bf16[512,2048]{1,0:T(8,128)(2,1)} async-done(((bf16[64,2048]{1,0:T(8,128)(2,1)}), bf16[512,2048]{1,0:T(8,128)(2,1)}) %all-gather.7.cloned.1.call-update) | async-done | bytes 2097168 | tf_op jit(solution)/shard_map/all_gather | solution.py:43
  41.7 3.4 fusion.54
  60.4 16.5 %all-gather.9.cloned.1.call-done = bf16[2048,2,128]{0,2,1:T(8,128)(2,1)} async-done(((bf16[512,2,128]{0,2,1:T(8,128)(2,1)}), bf16[2048,2,128]{0,2,1:T(8,128)(2,1)}) %all-gather.9.cloned.1.call-update) | async-done | bytes 1048592 | tf_op jit(solution)/shard_map/all_gather | solution.py:55
  82.3 23.6 %all-gather.11.cloned.1.call-done = bf16[2048,2,128]{0,2,1:T(8,128)(2,1)} async-done(((bf16[512,2,128]{0,2,1:T(8,128)(2,1)}), bf16[2048,2,128]{0,2,1:T(8,128)(2,1)}) %all-gather.11.cloned.1.call-update) | async-done | bytes 1048592 | tf_op jit(solution)/shard_map/all_gather | solution.py:56
  105.9 3.7 copy.32
  109.5 32.0 %while.37 = (s32[]{:T(128)}, f32[2,512]{1,0:T(2,128)S(1)}, f32[512,2,128]{0,2,1:T(8,128)}, bf16[4,512,2,128]{3,1,2,0:T(8,128)(2,1)}, bf16[512,2,128]{2,0,1:T(8,1...) while((s32[]{:T(128)}, f32[2,512]{1,0:T(2,128)S(1)}, ...), condition=%wide.region_6.7_spmd.clone, body=%wide.region_4.6_spmd.clone.sunk | while | flops 271844352 | bytes 8143544 | solution.py:75
  114.3 3.2 fusion.103
  122.3 3.2 fusion.103
  130.3 3.2 fusion.103
  138.3 3.2 fusion.103
  141.5 3.5 multiply_reduce_fusion.3
  151.2 33.2 %while.38 = (s32[]{:T(128)}, f32[512,2,128]{0,2,1:T(8,128)}, bf16[4,512,2,128]{1,3,2,0:T(8,128)(2,1)}, bf16[512,2,128]{2,1,0:T(2,128)(2,1)S(1)}, f32[2]{0:T(128)...) while((s32[]{:T(128)}, f32[512,2,128]{0,2,1:T(8,128)}, ...), condition=%wide.region_10.11_spmd.clone, body=%wide.region_9.10_spmd.clone.sunk | while | flops 406585344 | bytes 7087251 | solution.py:131
  155.9 3.6 fusion.110
  164.1 3.6 fusion.110
  172.4 3.8 fusion.110
  180.8 3.6 fusion.110
  190.8 13.2 %all_gather.33 = f32[2048,2]{0,1:T(2,128)S(1)} all-gather(f32[512,2]{0,1:T(2,128)S(1)} %get-tuple-element.734), channel_id=1, replica_groups=mesh['row'=4,'col'=8] {'row'}, dimensions={0}, use_global_device_ids=true | all-gather | bytes 20480 | tf_op jit(solution)/shard_map/all_gather | solution.py:137
  204.0 13.2 %all_gather.31 = f32[2048,2]{0,1:T(2,128)S(1)} all-gather(f32[512,2]{0,1:T(2,128)S(1)} %fusion.81), channel_id=1, replica_groups=mesh['row'=4,'col'=8] {'row'}, dimensions={0}, use_global_device_ids=true | all-gather | bytes 20480 | tf_op jit(solution)/shard_map/all_gather | solution.py:136
  217.2 3.4 convolution_convert_fusion.2
  220.9 36.4 %while.39 = (s32[]{:T(128)}, f32[512,2,128]{0,2,1:T(8,128)}, f32[512,2,128]{0,2,1:T(8,128)}, bf16[4,512,2,128]{3,1,0,2:T(8,128)(2,1)}, bf16[512,2,128]{2,0,1:T(8...) while((s32[]{:T(128)}, f32[512,2,128]{0,2,1:T(8,128)}, ...), condition=%wide.region_13.14_spmd.clone, body=%wide.region_12.13_spmd.clone.sunk | while | flops 541589504 | bytes 9988260 | solution.py:161
  226.7 3.2 fusion.118
  232.8 2.9 fusion.119
  235.8 3.3 fusion.118
  242.0 2.9 fusion.119
  244.9 3.3 fusion.118
  254.0 3.3 fusion.118
  262.7 4.3 %bitcast_convert_fusion.2 = bf16[512,2048]{1,0:T(8,128)(2,1)} fusion(bf16[3,2048,256]{2,1,0:T(8,128)(2,1)S(1)} %copy-done, bf16[1,512,256]{2,1,0:T(8,128)(2,1)} %copy.59, bf16[1,512,256]{2,1,0:T(8,128)(2,1)} %copy.58, bf16[1,512,256]{2,1,0:T(8,128)(2,1)} %stack_reshape.9), kind=kOutput, calls=%fused_computation.57 | convolution fusion | flops 1612447744 | bytes 6029312 | tf_op jit(solution)/shard_map/ksh,kdh->sd/dot_general | solution.py:184
  268.0 5.2 %fusion.50 = bf16[3,2048,256]{1,2,0:T(8,128)(2,1)} fusion(bf16[512,2048]{1,0:T(8,128)(2,1)} %all-gather.7.cloned.1.call-done, bf16[1,512,256]{2,1,0:T(8,128)(2,1)} %copy.59, bf16[1,512,256]{2,1,0:T(8,128)(2,1)} %copy.58, bf16[1,512,256]{2,1,0:T(8,128)(2,1)S(1)} %copy-done.11), kind=kOutput, calls=%fused_computation.60 | convolution fusion | flops 1612972032 | bytes 6029312 | tf_op jit(solution)/shard_map/sd,ksh->kdh/dot_general | solution.py:178
  274.2 3.4 convolution_convert_fusion.1
  279.5 28.2 %reduce-scatter.7.cloned.1.call-done = bf16[64,2048]{1,0:T(8,128)(2,1)} async-done(((bf16[512,2048]{1,0:T(8,128)(2,1)}), bf16[64,2048]{1,0:T(8,128)(2,1)}) %reduce-scatter.7.cloned.1.call-update) | async-done | bytes 262160 | tf_op jit(solution)/shard_map/reduce_scatter | solution.py:183
  310.8 59.7 %reduce-scatter.9.cloned.1.call-done = bf16[3,512,256]{1,2,0:T(8,128)(2,1)} async-done(((bf16[3,2048,256]{1,2,0:T(8,128)(2,1)}), bf16[3,512,256]{1,2,0:T(8,128)(2,1)}) %reduce-scatter.9.cloned.1.call-update) | async-done | bytes 786448 | tf_op jit(solution)/shard_map/reduce_scatter | solution.py:179
  373.0 42.2 %reduce-scatter.5.cloned.1.call-done = bf16[64,2048]{1,0:T(8,128)(2,1)} async-done(((bf16[512,2048]{1,0:T(8,128)(2,1)}), bf16[64,2048]{1,0:T(8,128)(2,1)}) %reduce-scatter.5.cloned.1.call-update) | async-done | bytes 262160 | tf_op jit(solution)/shard_map/reduce_scatter | solution.py:82
  (139 shorter events, 106.0 us)
Async XLA Ops:
  7.2 34.6 %copy-start = (bf16[3,2048,256]{2,1,0:T(8,128)(2,1)S(1)}, bf16[3,2048,256]{2,1,0:T(8,128)(2,1)}, u32[]{:S(2)}) copy-start(bf16[3,2048,256]{2,1,0:T(8,128)(2,1)} %param.16) | copy-start | bytes 9437188
  7.2 2.9 copy-start.7
  7.2 34.5 %all-gather.7.cloned.1.call-start = ((), (), s32[]{:S(2)}) async-start(), calls=%async_computation.4 | async-start | bytes 2359296 | tf_op jit(solution)/shard_map/all_gather | solution.py:43
  11.1 65.8 %all-gather.9.cloned.1.call-start = ((), (), s32[]{:S(2)}) async-start(), calls=%async_computation.5 | async-start | bytes 1310720 | tf_op jit(solution)/shard_map/all_gather | solution.py:55
  45.2 1.1 copy-start.10
  46.3 5.0 %copy-start.12 = (f32[2]{0:T(128)S(1)}, f32[2]{0:T(128)}, u32[]{:S(2)}) copy-start(f32[2]{0:T(128)} %param.17) | copy-start | bytes 28
  47.2 0.8 copy-start.4
  48.8 57.1 %all-gather.11.cloned.1.call-start = ((), (), s32[]{:S(2)}) async-start(), calls=%async_computation.6 | async-start | bytes 1310720 | tf_op jit(solution)/shard_map/all_gather | solution.py:56
  50.6 90.9 %all-gather.13.cloned.1.call-start = ((), (), s32[]{:S(2)}) async-start(), calls=%async_computation.8 | async-start | bytes 2359296 | tf_op jit(solution)/shard_map/all_gather | solution.py:88
  51.2 169.7 %all-gather.15.cloned.1.call-start = ((), (), s32[]{:S(2)}) async-start(), calls=%async_computation.9 | async-start | bytes 1310720 | tf_op jit(solution)/shard_map/all_gather | solution.py:140
  59.4 1.0 copy-start.1
  60.4 160.5 %all-gather.17.cloned.1.call-start = ((), (), s32[]{:S(2)}) async-start(), calls=%async_computation.10 | async-start | bytes 1310720 | tf_op jit(solution)/shard_map/all_gather | solution.py:141
  79.5 30.0 %copy-start.2 = (bf16[512,2,128]{2,0,1:T(8,128)(2,1)S(1)}, bf16[512,2,128]{2,0,1:T(8,128)(2,1)}, u32[]{:S(2)}) copy-start(bf16[512,2,128]{2,0,1:T(8,128)(2,1)} %copy-done.1) | copy-start | bytes 786436
  114.3 3.2 copy-start.3
  122.3 3.2 copy-start.3
  130.3 3.2 copy-start.3
  138.3 3.2 copy-start.3
  145.1 6.1 %copy-start.6 = (bf16[512,2,128]{2,1,0:T(2,128)(2,1)S(1)}, bf16[512,2,128]{2,1,0:T(2,128)(2,1)}, u32[]{:S(2)}) copy-start(bf16[512,2,128]{2,1,0:T(2,128)(2,1)} %copy.36) | copy-start | bytes 786436
  151.2 126.4 %reduce-scatter.11.cloned.1.call-start = ((), (), s32[]{:S(2)}) async-start(), calls=%async_computation.13 | async-start | bytes 1310720 | tf_op jit(solution)/shard_map/reduce_scatter | solution.py:92
  217.2 3.7 copy-start.5
  220.7 87.1 %reduce-scatter.7.cloned.1.call-start = ((), (), s32[]{:S(2)}) async-start(), calls=%async_computation.11 | async-start | bytes 2359296 | tf_op jit(solution)/shard_map/reduce_scatter | solution.py:183
  267.0 0.9 copy-start.11
  267.1 103.4 %reduce-scatter.9.cloned.1.call-start = ((), (), s32[]{:S(2)}) async-start(), calls=%async_computation.12 | async-start | bytes 3932160 | tf_op jit(solution)/shard_map/reduce_scatter | solution.py:179
  273.2 1.0 copy-start.9
  273.3 142.0 %reduce-scatter.5.cloned.1.call-start = ((), (), s32[]{:S(2)}) async-start(), calls=%async_computation.7 | async-start | bytes 2359296 | tf_op jit(solution)/shard_map/reduce_scatter | solution.py:82
  277.6 30.2 %copy-start.8 = (bf16[64,2048]{1,0:T(8,128)(2,1)S(1)}, bf16[64,2048]{1,0:T(8,128)(2,1)}, u32[]{:S(2)}) copy-start(bf16[64,2048]{1,0:T(8,128)(2,1)} %param.13) | copy-start | bytes 786436
Sparse Core Ops, SparseCore 0:
  11.2 30.4 all-gather.6
  48.9 27.9 all-gather.8
  78.5 27.3 all-gather.10
  107.6 27.1 all-gather.12
  136.8 28.0 all-gather.14
  166.3 27.3 all-gather.16
  220.8 26.5 reduce-scatter.10
  267.2 40.4 reduce-scatter.6
  310.0 60.3 reduce-scatter.8
  374.2 41.0 reduce-scatter.4
where the time goes:
time: 424 us; the launch traced here: 422 us
  waiting for transfers between devices  202 us (48%)
  matrix products  109 us (26%)
  local copies, waits for them, and re-layouts  50.9 us (12%)
  blocking collectives  26.4 us (6%)
  other arithmetic  17.9 us (4%)
  between operations  15.3 us (4%)
    reduce_scatter x1, waiting for transfers between devices, per_device(): lax.psum_scatter(qkv_part.astype(jnp.bfloat16), 'row', scatter_dimension=...  59.7 us
    reduce_scatter x1, waiting for transfers between devices, per_device(): lax.psum_scatter(jnp.dot(rows, out_weight, preferred_element_type=jnp.flo...  42.2 us
    all_gather x1, waiting for transfers between devices, per_device(): group = lax.all_gather(hidden, 'col', axis=0, tiled=True)  30.6 us
    reduce_scatter x1, waiting for transfers between devices, per_device(): lax.psum_scatter(jnp.einsum('ksh,kdh->sd', rows, qkv_weight, preferred_el...  28.2 us
    all_gather x1, waiting for transfers between devices, per_device(): value_piece = lax.all_gather(value_heads, 'row', axis=0, tiled=True)  23.6 us
    dot_general x8, matrix products, pair_terms(): jnp.einsum('qhd,khd->hqk', query_rows, key_block, preferred_element_type=...  22.8 us
    all_gather x1, waiting for transfers between devices, per_device(): key_piece = lax.all_gather(key_heads, 'row', axis=0, tiled=True)  16.5 us
    unnamed x30, local copies, waits for them, and re-layouts  15.4 us
  transfers between devices with their start and end apart: 10, of which 6 were waited for; matrix products, arithmetic and copies ran while one was open for 39% of the time, Pallas kernels for 0%

commit v1 on v0

--- a/solution.py
+++ b/solution.py
@@ -53,7 +53,12 @@
     )
     carry = start_state
     key_piece = lax.all_gather(key_heads, "row", axis=0, tiled=True)
-    value_piece = lax.all_gather(value_heads, "row", axis=0, tiled=True)
+    ring = [value_heads]
+    for hop in range(3):
+        ring.append(lax.ppermute(ring[-1], "row", [(dev, (dev + 1) % 4) for dev in range(4)]))
+    value_piece = jnp.roll(
+        jnp.concatenate(ring[::-1], axis=0), (lax.axis_index("row") + 1) * ring[0].shape[0], axis=0
+    )
     size = math.gcd(key_piece.shape[0], 512)
 
     def attend_step(state, block):

time: 424 us -> 420 us (level)
  waiting for transfers between devices: 202 us -> 194 us
  starting transfers between devices: 0.59 us -> 4.88 us
    ppermute x0 -> x3, waiting for transfers between devices: none -> 29.1 us  [per_device(): lax.ppermute(ring[-1], 'row', [(dev, (dev + 1) % 4) for dev in range(4)])]
    all_gather x1, waiting for transfers between devices: 23.6 us -> 3.61 us  [per_device(): value_piece = lax.all_gather(value_heads, 'row', axis=0, tiled=True)]
    all_gather x1, waiting for transfers between devices: 16.5 us -> 0.01 us  [per_device(): key_piece = lax.all_gather(key_heads, 'row', axis=0, tiled=True)]
    dynamic_slice x8 -> x1, local copies, waits for them, and re-layouts: 8 us -> 1.05 us  [per_device(): jnp.roll(jnp.concatenate(ring[::-1], axis=0), (lax.axis_index('row') + 1)...]
    unnamed x30 -> x41, local copies, waits for them, and re-layouts: 15.4 us -> 20.3 us
    ppermute x0 -> x3, starting transfers between devices: none -> 4.29 us  [per_device(): lax.ppermute(ring[-1], 'row', [(dev, (dev + 1) % 4) for dev in range(4)])]
  transfers between devices with their start and end apart: 10 -> 13, of which waited for: 6 -> 8; matrix products, arithmetic and copies ran while one was open for 39% -> 39% of each run, Pallas kernels for 0% -> 0%
where the time goes in v1:
time: 420 us; the launch traced here: 418 us
  waiting for transfers between devices  194 us (46%)
  matrix products  109 us (26%)
  local copies, waits for them, and re-layouts  49.8 us (12%)
  blocking collectives  26.7 us (6%)
  other arithmetic  17.9 us (4%)
  between operations  15.2 us (4%)
  starting transfers between devices  4.88 us (1%)
    reduce_scatter x1, waiting for transfers between devices, per_device(): lax.psum_scatter(qkv_part.astype(jnp.bfloat16), 'row', scatter_dimension=...  59.7 us
    reduce_scatter x1, waiting for transfers between devices, per_device(): lax.psum_scatter(jnp.dot(rows, out_weight, preferred_element_type=jnp.flo...  42.2 us
    all_gather x1, waiting for transfers between devices, per_device(): group = lax.all_gather(hidden, 'col', axis=0, tiled=True)  30.6 us
    ppermute x3, waiting for transfers between devices, per_device(): lax.ppermute(ring[-1], 'row', [(dev, (dev + 1) % 4) for dev in range(4)])  29.1 us
    reduce_scatter x1, waiting for transfers between devices, per_device(): lax.psum_scatter(jnp.einsum('ksh,kdh->sd', rows, qkv_weight, preferred_el...  28.3 us
    dot_general x8, matrix products, pair_terms(): jnp.einsum('qhd,khd->hqk', query_rows, key_block, preferred_element_type=...  22.7 us
    unnamed x41, local copies, waits for them, and re-layouts  20.3 us
    dot_general x4, matrix products, query_step(): jnp.einsum('hqk,khd->qhd', dscores, key_block, preferred_element_type=jnp...  14.6 us
  transfers between devices with their start and end apart: 13, of which 8 were waited for; matrix products, arithmetic and copies ran while one was open for 39% of the time, Pallas kernels for 0%

profile of v1, /device:TPU:0, one launch (start us, length us, event | category | flops | bytes accessed | tf_op | source)
XLA Modules:
  0.0 418.0 jit_solution(6942737748760502146)
XLA Ops:
  11.1 30.6 %all-gather.7.cloned.1.call-done = bf16[512,2048]{1,0:T(8,128)(2,1)} async-done(((bf16[64,2048]{1,0:T(8,128)(2,1)}), bf16[512,2048]{1,0:T(8,128)(2,1)}) %all-gather.7.cloned.1.call-update) | async-done | bytes 2097168 | tf_op jit(solution)/shard_map/all_gather | solution.py:43
  41.7 3.4 fusion.56
  54.8 12.6 %collective-permute-done = bf16[512,2,128]{2,0,1:T(8,128)(2,1)} collective-permute-done((bf16[512,2,128]{2,0,1:T(8,128)(2,1)}, bf16[512,2,128]{2,0,1:T(8,128)(2,1)}, u32[]{:S(2)}, u32[]{:S(2)}) %collective-permute-start) | collective-permute-done | bytes 262176 | tf_op jit(solution)/shard_map/ppermute | solution.py:58
  71.3 15.1 %collective-permute-done.1 = bf16[512,2,128]{2,0,1:T(8,128)(2,1)} collective-permute-done((bf16[512,2,128]{2,0,1:T(8,128)(2,1)}, bf16[512,2,128]{2,0,1:T(8,128)(2,1)}, u32[]{:S(2)}, u32[]{:S(2)}) %collective-permute-start.1) | collective-permute-done | bytes 262176 | tf_op jit(solution)/shard_map/ppermute | solution.py:58
  108.2 23.6 %while.37 = (s32[]{:T(128)}, f32[2,512]{1,0:T(2,128)S(1)}, f32[512,2,128]{0,2,1:T(8,128)}, bf16[4,512,2,128]{3,1,2,0:T(8,128)(2,1)}, bf16[512,2,128]{2,0,1:T(8,1...) while((s32[]{:T(128)}, f32[2,512]{1,0:T(2,128)S(1)}, ...), condition=%wide.region_6.7_spmd.clone, body=%wide.region_4.6_spmd.clone.sunk | while | flops 271844352 | bytes 6046864 | solution.py:80
  111.0 3.1 fusion.105
  116.8 3.1 fusion.105
  122.7 3.2 fusion.105
  128.6 3.1 fusion.105
  131.8 3.4 multiply_reduce_fusion.3
  139.4 3.6 all-gather.11.cloned.1.call-done
  143.0 3.7 copy.36
  146.7 33.2 %while.38 = (s32[]{:T(128)}, f32[512,2,128]{0,2,1:T(8,128)}, bf16[4,512,2,128]{1,3,2,0:T(8,128)(2,1)}, bf16[512,2,128]{2,1,0:T(2,128)(2,1)S(1)}, f32[2]{0:T(128)...) while((s32[]{:T(128)}, f32[512,2,128]{0,2,1:T(8,128)}, ...), condition=%wide.region_10.11_spmd.clone, body=%wide.region_9.10_spmd.clone.sunk | while | flops 406585344 | bytes 7087251 | solution.py:136
  151.3 3.7 fusion.112
  159.7 3.7 fusion.112
  168.0 3.6 fusion.112
  176.2 3.6 fusion.112
  186.2 13.5 %all_gather.32 = f32[2048,2]{0,1:T(2,128)S(1)} all-gather(f32[512,2]{0,1:T(2,128)S(1)} %get-tuple-element.726), channel_id=1, replica_groups=mesh['row'=4,'col'=8] {'row'}, dimensions={0}, use_global_device_ids=true | all-gather | bytes 20480 | tf_op jit(solution)/shard_map/all_gather | solution.py:142
  199.7 13.2 %all_gather.30 = f32[2048,2]{0,1:T(2,128)S(1)} all-gather(f32[512,2]{0,1:T(2,128)S(1)} %fusion.83), channel_id=1, replica_groups=mesh['row'=4,'col'=8] {'row'}, dimensions={0}, use_global_device_ids=true | all-gather | bytes 20480 | tf_op jit(solution)/shard_map/all_gather | solution.py:141
  212.9 3.4 convolution_convert_fusion.2
  216.7 36.4 %while.39 = (s32[]{:T(128)}, f32[512,2,128]{0,2,1:T(8,128)}, f32[512,2,128]{0,2,1:T(8,128)}, bf16[4,512,2,128]{3,1,0,2:T(8,128)(2,1)}, bf16[512,2,128]{2,0,1:T(8...) while((s32[]{:T(128)}, f32[512,2,128]{0,2,1:T(8,128)}, ...), condition=%wide.region_13.14_spmd.clone, body=%wide.region_12.13_spmd.clone.sunk | while | flops 541589504 | bytes 9988260 | solution.py:166
  222.5 3.2 fusion.120
  228.6 3.0 fusion.121
  231.5 3.3 fusion.120
  240.7 3.3 fusion.120
  249.8 3.3 fusion.120
  258.5 4.3 %bitcast_convert_fusion.2 = bf16[512,2048]{1,0:T(8,128)(2,1)} fusion(bf16[3,2048,256]{2,1,0:T(8,128)(2,1)S(1)} %copy-done, bf16[1,512,256]{2,1,0:T(8,128)(2,1)} %copy.61, bf16[1,512,256]{2,1,0:T(8,128)(2,1)} %copy.60, bf16[1,512,256]{2,1,0:T(8,128)(2,1)} %stack_reshape.9), kind=kOutput, calls=%fused_computation.58 | convolution fusion | flops 1612447744 | bytes 6029312 | tf_op jit(solution)/shard_map/ksh,kdh->sd/dot_general | solution.py:189
  263.8 5.3 %fusion.52 = bf16[3,2048,256]{1,2,0:T(8,128)(2,1)} fusion(bf16[512,2048]{1,0:T(8,128)(2,1)} %all-gather.7.cloned.1.call-done, bf16[1,512,256]{2,1,0:T(8,128)(2,1)} %copy.61, bf16[1,512,256]{2,1,0:T(8,128)(2,1)} %copy.60, bf16[1,512,256]{2,1,0:T(8,128)(2,1)S(1)} %copy-done.12), kind=kOutput, calls=%fused_computation.61 | convolution fusion | flops 1612972032 | bytes 6029312 | tf_op jit(solution)/shard_map/sd,ksh->kdh/dot_general | solution.py:183
  270.0 3.4 convolution_convert_fusion.1
  275.3 28.3 %reduce-scatter.7.cloned.1.call-done = bf16[64,2048]{1,0:T(8,128)(2,1)} async-done(((bf16[512,2048]{1,0:T(8,128)(2,1)}), bf16[64,2048]{1,0:T(8,128)(2,1)}) %reduce-scatter.7.cloned.1.call-update) | async-done | bytes 262160 | tf_op jit(solution)/shard_map/reduce_scatter | solution.py:188
  306.7 59.7 %reduce-scatter.9.cloned.1.call-done = bf16[3,512,256]{1,2,0:T(8,128)(2,1)} async-done(((bf16[3,2048,256]{1,2,0:T(8,128)(2,1)}), bf16[3,512,256]{1,2,0:T(8,128)(2,1)}) %reduce-scatter.9.cloned.1.call-update) | async-done | bytes 786448 | tf_op jit(solution)/shard_map/reduce_scatter | solution.py:184
  368.9 42.2 %reduce-scatter.5.cloned.1.call-done = bf16[64,2048]{1,0:T(8,128)(2,1)} async-done(((bf16[512,2048]{1,0:T(8,128)(2,1)}), bf16[64,2048]{1,0:T(8,128)(2,1)}) %reduce-scatter.5.cloned.1.call-update) | async-done | bytes 262160 | tf_op jit(solution)/shard_map/reduce_scatter | solution.py:87
  (143 shorter events, 113.7 us)
Async XLA Ops:
  7.2 34.6 %copy-start = (bf16[3,2048,256]{2,1,0:T(8,128)(2,1)S(1)}, bf16[3,2048,256]{2,1,0:T(8,128)(2,1)}, u32[]{:S(2)}) copy-start(bf16[3,2048,256]{2,1,0:T(8,128)(2,1)} %param.16) | copy-start | bytes 9437188
  7.2 2.9 copy-start.6
  7.2 34.5 %all-gather.7.cloned.1.call-start = ((), (), s32[]{:S(2)}) async-start(), calls=%async_computation.4 | async-start | bytes 2359296 | tf_op jit(solution)/shard_map/all_gather | solution.py:43
  11.1 91.8 %all-gather.9.cloned.1.call-start = ((), (), s32[]{:S(2)}) async-start(), calls=%async_computation.5 | async-start | bytes 1310720 | tf_op jit(solution)/shard_map/all_gather | solution.py:55
  45.2 1.1 copy-start.11
  47.2 0.8 copy-start.3
  47.2 23.0 %copy-start.13 = (f32[2]{0:T(128)S(1)}, f32[2]{0:T(128)}, u32[]{:S(2)}) copy-start(f32[2]{0:T(128)} %param.17) | copy-start | bytes 28
  48.8 83.0 %all-gather.13.cloned.1.call-start = ((), (), s32[]{:S(2)}) async-start(), calls=%async_computation.8 | async-start | bytes 2359296 | tf_op jit(solution)/shard_map/all_gather | solution.py:93
  49.5 93.5 %all-gather.11.cloned.1.call-start = ((), (), s32[]{:S(2)}) async-start(), calls=%async_computation.7 | async-start | bytes 1310720 | tf_op jit(solution)/shard_map/all_gather | solution.py:124
  51.4 38.9 %copy-start.8 = (bf16[1,512,256]{1,2,0:T(8,128)(2,1)S(1)}, bf16[1,512,256]{1,2,0:T(8,128)(2,1)}, u32[]{:S(2)}) copy-start(bf16[1,512,256]{1,2,0:T(8,128)(2,1)} %slice.17) | copy-start | bytes 786436
  51.4 165.2 %all-gather.15.cloned.1.call-start = ((), (), s32[]{:S(2)}) async-start(), calls=%async_computation.9 | async-start | bytes 1310720 | tf_op jit(solution)/shard_map/all_gather | solution.py:145
  53.3 14.1 %collective-permute-start = (bf16[512,2,128]{2,0,1:T(8,128)(2,1)}, bf16[512,2,128]{2,0,1:T(8,128)(2,1)}, u32[]{:S(2)}, u32[]{:S(2)}) collective-permute-start(bf16[512,2,128]{2,0,1:T(8,128)(2,1)} %copy.31), channel_id=1, source_target_pairs={{0,8},{8,16},{16,24},{24,0},{1,9},{9,17},{17,25},{25,1},{2,10},{10... | collective-permute-start | bytes 786440 | tf_op jit(solution)/shard_map/ppermute | solution.py:58
  67.4 19.0 %collective-permute-start.1 = (bf16[512,2,128]{2,0,1:T(8,128)(2,1)}, bf16[512,2,128]{2,0,1:T(8,128)(2,1)}, u32[]{:S(2)}, u32[]{:S(2)}) collective-permute-start(bf16[512,2,128]{2,0,1:T(8,128)(2,1)} %collective-permute-done), channel_id=1, source_target_pairs={{0,8},{8,16},{16,24},{24,0},{1,9},{9,17},{17,25},{25,1},{2,10},{10... | collective-permute-start | bytes 786440 | tf_op jit(solution)/shard_map/ppermute | solution.py:58
  86.4 8.5 %collective-permute-start.2 = (bf16[512,2,128]{2,0,1:T(8,128)(2,1)}, bf16[512,2,128]{2,0,1:T(8,128)(2,1)}, u32[]{:S(2)}, u32[]{:S(2)}) collective-permute-start(bf16[512,2,128]{2,0,1:T(8,128)(2,1)} %collective-permute-done.1), channel_id=1, source_target_pairs={{0,8},{8,16},{16,24},{24,0},{1,9},{9,17},{17,25},{25,1},{2,10},{10... | collective-permute-start | bytes 786440 | tf_op jit(solution)/shard_map/ppermute | solution.py:58
  92.4 1.0 copy-start.1
  93.4 8.4 %copy-start.10 = (bf16[512,2,128]{2,0,1:T(8,128)(2,1)S(1)}, bf16[512,2,128]{2,0,1:T(8,128)(2,1)}, u32[]{:S(2)}) copy-start(bf16[512,2,128]{2,0,1:T(8,128)(2,1)} %copy.31) | copy-start | bytes 786436
  93.4 123.2 %all-gather.17.cloned.1.call-start = ((), (), s32[]{:S(2)}) async-start(), calls=%async_computation.10 | async-start | bytes 1310720 | tf_op jit(solution)/shard_map/all_gather | solution.py:146
  102.9 5.3 %copy-start.2 = (bf16[512,2,128]{2,0,1:T(8,128)(2,1)S(1)}, bf16[512,2,128]{2,0,1:T(8,128)(2,1)}, u32[]{:S(2)}) copy-start(bf16[512,2,128]{2,0,1:T(8,128)(2,1)} %copy-done.1) | copy-start | bytes 786436
  137.0 9.7 %copy-start.5 = (bf16[512,2,128]{2,1,0:T(2,128)(2,1)S(1)}, bf16[512,2,128]{2,1,0:T(2,128)(2,1)}, u32[]{:S(2)}) copy-start(bf16[512,2,128]{2,1,0:T(2,128)(2,1)} %copy.38) | copy-start | bytes 786436
  139.3 134.1 %reduce-scatter.11.cloned.1.call-start = ((), (), s32[]{:S(2)}) async-start(), calls=%async_computation.13 | async-start | bytes 1310720 | tf_op jit(solution)/shard_map/reduce_scatter | solution.py:97
  212.9 3.7 copy-start.4
  216.4 87.3 %reduce-scatter.7.cloned.1.call-start = ((), (), s32[]{:S(2)}) async-start(), calls=%async_computation.11 | async-start | bytes 2359296 | tf_op jit(solution)/shard_map/reduce_scatter | solution.py:188
  262.8 0.9 copy-start.12
  262.8 103.5 %reduce-scatter.9.cloned.1.call-start = ((), (), s32[]{:S(2)}) async-start(), calls=%async_computation.12 | async-start | bytes 3932160 | tf_op jit(solution)/shard_map/reduce_scatter | solution.py:184
  269.0 1.0 copy-start.9
  269.1 142.1 %reduce-scatter.5.cloned.1.call-start = ((), (), s32[]{:S(2)}) async-start(), calls=%async_computation.6 | async-start | bytes 2359296 | tf_op jit(solution)/shard_map/reduce_scatter | solution.py:87
  273.4 30.2 %copy-start.7 = (bf16[64,2048]{1,0:T(8,128)(2,1)S(1)}, bf16[64,2048]{1,0:T(8,128)(2,1)}, u32[]{:S(2)}) copy-start(bf16[64,2048]{1,0:T(8,128)(2,1)} %param.13) | copy-start | bytes 786436
Sparse Core Ops, SparseCore 0:
  11.2 30.4 all-gather.6
  48.9 37.5 all-gather.8
  88.4 25.0 all-gather.12
  115.0 27.9 all-gather.10
  145.0 27.3 all-gather.14
  173.8 27.6 all-gather.16
  216.5 26.6 reduce-scatter.10
  263.0 40.6 reduce-scatter.6
  306.0 60.3 reduce-scatter.8
  370.1 41.0 reduce-scatter.4
